TPU v7x, 256 devices: a whole 4x4x8 slice. The times are simulated.
256 devices in a mesh: cand: 16 (over z_hi, x, core), seq: 16 (over z_lo, y).
Axes of the slice: x: 4, y: 4, z: 8 (z_hi: 2, z_lo: 4; z = z_hi * 4 + z_lo), core: 2. Of those that a mesh axis runs over, the one named last changes fastest.
Arguments:
- latent: bfloat16 [16, 768, 3072], P('cand', 'seq'), may hold values from -0.59765625 to 0.59765625
- timesteps: int32 [16], replicated, may hold values from 0 to 999
- positions: int32 [3, 768], replicated, may hold values from 0 to 63
- mod_weight: bfloat16 [3072, 9216], P('cand', 'seq'), may hold values from -0.109375 to 0.109375
- input_weight: bfloat16 [3072, 16, 384], P('cand', 'seq'), may hold values from -0.109375 to 0.109375
- output_weight: bfloat16 [16, 128, 3072], P('seq', None, 'cand'), may hold values from -0.75 to 0.75
- cotangent: bfloat16 [16, 768, 3072], P('cand', 'seq'), may hold values from -6 to 6
Outputs:
- block_out: bfloat16 [16, 768, 3072], P('cand', 'seq')
- latent_grad: float32 [16, 768, 3072], P('cand', 'seq')
All inputs are finite; a program needn't handle non-finite values.
Results may differ from a plain program's by a relative error of at most 0.033.
Values may be sent and summed in bfloat16 or wider, within the bound.
No kernel may reach another device: no remote copies, remote signals or barrier semaphores. Data moves between devices by JAX's collectives and lax.ppermute only.
A program may use at most 128 MiB of HBM per device.

v0:
```python
import jax
import jax.numpy as jnp
import numpy as np
from jax import lax
from jax.sharding import PartitionSpec as P

HEAD = 128
epsilon = 1e-06


def in_blocks(value, dim, size):
    dims = value.shape
    parts = value.reshape(*dims[:dim], size, dims[dim] // size, *dims[dim + 1 :])
    return jnp.moveaxis(parts, dim, 0)


def summed_on_arrival(value, axis, dim):
    size = lax.axis_size(axis)
    parts = lax.all_to_all(in_blocks(value, dim, size), axis, 0, 0, tiled=True)
    return jnp.sum(parts.astype(jnp.float32), axis=0)


def in_order(parts, dim):
    parts = jnp.moveaxis(parts, 0, dim)
    dims = parts.shape
    return parts.reshape(*dims[:dim], dims[dim] * dims[dim + 1], *dims[dim + 2 :])


def from_everyone(value, axis):
    copies = jnp.broadcast_to(value, (lax.axis_size(axis), *value.shape))
    return lax.all_to_all(copies, axis, split_axis=0, concat_axis=0, tiled=True)


def gathered_copies(value, axis, dim):
    return in_order(from_everyone(value, axis), dim)


def time_embed(timesteps, feature_width):
    half_size = feature_width // 2
    freq_rate = jnp.exp(-jnp.log(10000.0) * jnp.arange(half_size, dtype=jnp.float32) / half_size)
    angles = timesteps.astype(jnp.float32)[:, None] * freq_rate[None, :]
    return jnp.concatenate([jnp.cos(angles), jnp.sin(angles)], axis=1)


def rope_tables(positions, head_size):
    first_size = head_size // 8
    other_size = (head_size - first_size) // 2
    pieces = []
    swapped = []
    sign_vec = []
    offset = 0
    for axis_id, width_part in enumerate((first_size, other_size, other_size)):
        half_size = width_part // 2
        freq_rate = jnp.exp(
            -jnp.log(256.0) * 2.0 * jnp.arange(half_size, dtype=jnp.float32) / width_part
        )
        angle_part = positions[axis_id].astype(jnp.float32)[:, None] * freq_rate[None, :]
        pieces.append(angle_part)
        pieces.append(angle_part)
        swapped += list(range(offset + half_size, offset + width_part)) + list(
            range(offset, offset + half_size)
        )
        sign_vec += [-1.0] * half_size + [1.0] * half_size
        offset += width_part
    angles = jnp.concatenate(pieces, axis=1)
    return (
        jnp.cos(angles),
        jnp.sin(angles),
        np.array(swapped, np.int32),
        np.array(sign_vec, np.float32),
    )


def rotate(values, tables):
    cos_tab, sin_tab, swapped, sign_vec = tables
    return values * cos_tab + values[..., swapped] * sign_vec * sin_tab


def unrotate(values, tables):
    cos_tab, sin_tab, swapped, sign_vec = tables
    return values * cos_tab - (values * sin_tab)[..., swapped] * sign_vec


def rms_norm(values):
    inverse = lax.rsqrt(jnp.mean(values * values, -1, keepdims=True) + epsilon)
    return (values * inverse, inverse)


def rms_back(d_normed, normed, inverse):
    return inverse * (d_normed - normed * jnp.mean(d_normed * normed, -1, keepdims=True))


def layer_norm(values):
    centred = values - jnp.mean(values, -1, keepdims=True)
    inverse_std = lax.rsqrt(jnp.mean(centred * centred, -1, keepdims=True) + epsilon)
    return (centred * inverse_std, inverse_std)


def layer_norm_back(d_normed, normed, inverse_std):
    return inverse_std * (
        d_normed
        - jnp.mean(d_normed, -1, keepdims=True)
        - normed * jnp.mean(d_normed * normed, -1, keepdims=True)
    )


def times_transposed(left, right):
    return lax.dot_general(
        left, right, (((1,), (1,)), ((), ())), preferred_element_type=jnp.float32
    )


def attend(projected, tables):
    length, groups, triple = projected.shape
    head_size = triple // 3
    grouped = jnp.transpose(projected.reshape(length, groups, 3, head_size), (2, 1, 0, 3))
    query_n, query_inv = rms_norm(grouped[0])
    key_n, key_inv = rms_norm(grouped[1])
    q_rot = rotate(query_n, tables).astype(jnp.bfloat16)
    k_rot = rotate(key_n, tables).astype(jnp.bfloat16)
    values = grouped[2].astype(jnp.bfloat16)
    score_scale = head_size ** (-0.5)
    scores = (
        jnp.einsum("gld,gmd->glm", q_rot, k_rot, preferred_element_type=jnp.float32) * score_scale
    )
    weights = jnp.exp(scores - head_size**0.5)
    probs = weights / jnp.sum(weights, -1, keepdims=True)
    probs_low = probs.astype(jnp.bfloat16)
    heads_out = jnp.einsum("glm,gmd->gld", probs_low, values, preferred_element_type=jnp.float32)
    attended = (
        jnp.transpose(heads_out, (1, 0, 2)).reshape(length, groups * head_size).astype(jnp.bfloat16)
    )
    saved = (q_rot, k_rot, values, probs, probs_low, query_n, query_inv, key_n, key_inv)
    return (attended, saved)


def attend_back(d_attended, saved, tables):
    q_rot, k_rot, values, probs, probs_low, query_n, query_inv, key_n, key_inv = saved
    groups, length, head_size = q_rot.shape
    score_scale = head_size ** (-0.5)
    d_heads = jnp.transpose(d_attended.reshape(length, groups, head_size), (1, 0, 2))
    d_values = jnp.einsum("glm,gld->gmd", probs_low, d_heads, preferred_element_type=jnp.float32)
    d_probs = jnp.einsum("gld,gmd->glm", d_heads, values, preferred_element_type=jnp.float32)
    d_scores = (probs * (d_probs - jnp.sum(probs * d_probs, -1, keepdims=True))).astype(
        jnp.bfloat16
    )
    d_qrot = (
        jnp.einsum("glm,gmd->gld", d_scores, k_rot, preferred_element_type=jnp.float32)
        * score_scale
    )
    d_krot = (
        jnp.einsum("glm,gld->gmd", d_scores, q_rot, preferred_element_type=jnp.float32)
        * score_scale
    )
    d_query = rms_back(unrotate(d_qrot, tables), query_n, query_inv)
    d_key = rms_back(unrotate(d_krot, tables), key_n, key_inv)
    stacked = jnp.stack([d_query, d_key, d_values], 0)
    return (
        jnp.transpose(stacked, (2, 1, 0, 3))
        .reshape(length, groups * 3 * head_size)
        .astype(jnp.bfloat16)
    )


def on_device(latent, timesteps, positions, mod_weight, input_weight, output_weight, cotangent):
    width = latent.shape[2]
    rows_local = latent.shape[1]
    groups = input_weight.shape[1]
    group_cols = groups * input_weight.shape[2]
    time_act = jax.nn.silu(time_embed(timesteps, width)).astype(jnp.bfloat16)
    slab_rows = mod_weight.shape[0]
    act_rows = lax.dynamic_slice_in_dim(time_act, lax.axis_index("cand") * slab_rows, slab_rows, 1)
    mod_mine = summed_on_arrival(
        jnp.dot(act_rows, mod_weight, preferred_element_type=jnp.float32).astype(jnp.bfloat16),
        "cand",
        0,
    )
    modulation = gathered_copies(mod_mine, "seq", 1)[0]
    shift_vec = modulation[:width]
    scale_vec = modulation[width : 2 * width]
    gate_vec = modulation[2 * width :]
    latent_rows = latent[0].astype(jnp.float32)
    normed, inverse_std = layer_norm(latent_rows)
    modulated = (normed * (1.0 + scale_vec) + shift_vec).astype(jnp.bfloat16)
    gathered = lax.all_gather(modulated, "seq", axis=0, tiled=True)
    length = gathered.shape[0]
    tables = rope_tables(positions, HEAD)
    w_full = lax.all_gather(input_weight, "cand", axis=0, tiled=True).reshape(width, group_cols)
    projected = jnp.dot(gathered, w_full, preferred_element_type=jnp.float32)
    attended, saved = attend(projected.reshape(length, groups, 3 * HEAD), tables)
    w_heads = gathered_copies(output_weight, "seq", 0)
    w_all = lax.all_gather(w_heads, "cand", axis=2, tiled=True)
    w_all = w_all.reshape(w_all.shape[0] * w_all.shape[1], width)
    token_heads = lax.all_to_all(attended, "seq", split_axis=0, concat_axis=1, tiled=True)
    mixed = jnp.dot(token_heads, w_all, preferred_element_type=jnp.float32)
    block_out = (latent_rows + gate_vec * mixed).astype(jnp.bfloat16)
    d_mixed = (cotangent[0].astype(jnp.float32) * gate_vec).astype(jnp.bfloat16)
    d_tokens = times_transposed(d_mixed, w_all).astype(jnp.bfloat16)
    d_attended = lax.all_to_all(d_tokens, "seq", split_axis=1, concat_axis=0, tiled=True)
    d_projected = attend_back(d_attended, saved, tables)
    d_modulated = lax.psum_scatter(
        times_transposed(
            lax.slice_in_dim(d_projected, 0, rows_local * lax.axis_size("seq"), axis=0), w_full
        ).astype(jnp.bfloat16),
        "seq",
        scatter_dimension=0,
        tiled=True,
    ).astype(jnp.float32)
    latent_grad = cotangent[0].astype(jnp.float32) + layer_norm_back(
        d_modulated * (1.0 + scale_vec), normed, inverse_std
    )
    return (block_out[None], latent_grad[None])


def solution(mesh):
    placed = (
        P("cand", "seq", None),
        P(),
        P(),
        P("cand", "seq"),
        P("cand", "seq", None),
        P("seq", None, "cand"),
        P("cand", "seq", None),
    )
    return jax.shard_map(
        on_device,
        mesh=mesh,
        in_specs=placed,
        out_specs=(P("cand", "seq", None), P("cand", "seq", None)),
        check_vma=False,
    )
```

profile of v0, /device:TPU:4, one launch (start us, length us, event | category | flops | bytes accessed | tf_op | source)
XLA Modules:
  0.0 455.1 jit_solution(4602630234816793834)
XLA Ops:
  7.2 0.0 all-gather.7.cloned.1.call-start
  7.2 0.7 all-gather.7.cloned.1.call-update
  7.9 0.7 convert_element_type.131
  8.6 0.4 multiply_cosine_fusion
  9.0 0.2 fusion.32
  9.3 0.5 broadcast.530
  9.8 0.7 reduce.19
  10.5 0.7 reshape.1012
  11.2 11.4 %all-to-all-start = ((bf16[16,2,288]{2,1,0:T(2,128)(2,1)}), bf16[16,2,288]{2,1,0:T(2,128)(2,1)S(1)}, u32[]{:S(2)}, u32[]{:S(2)}) async-start(bf16[16,2,288]{2,1,0:T(2,128)(2,1)} %reshape.1012), calls=%async_computation | async-start | bytes 49152 | tf_op jit(solution)/shard_map/all_to_all | solution.py:19
  22.6 1.1 convert_reduce_fusion
  23.7 1.2 fusion.46
  24.9 5.4 %all-to-all-done = bf16[16,2,288]{2,1,0:T(2,128)(2,1)S(1)} async-done(((bf16[16,2,288]{2,1,0:T(2,128)(2,1)}), bf16[16,2,288]{2,1,0:T(2,128)(2,1)S(1)}, u32[]{:S(2)}, u32[]{:S(2)}) %all-to-all-start) | async-done | bytes 18464 | tf_op jit(solution)/shard_map/all_to_all | solution.py:19
  30.4 0.1 reshape.1013
  30.5 0.1 convert_reduce_fusion.1
  30.5 0.6 broadcast_in_dim.16
  31.2 6.0 %all-to-all-start.1 = ((f32[16,1,576]{2,1,0:T(1,128)}), f32[16,1,576]{2,1,0:T(1,128)S(1)}, u32[]{:S(2)}, u32[]{:S(2)}) async-start(f32[16,1,576]{2,1,0:T(1,128)} %broadcast_in_dim.16), calls=%async_computation.1 | async-start | bytes 81920 | tf_op jit(solution)/shard_map/all_to_all | solution.py:31
  37.2 0.0 all-gather.5.cloned.1.call-start
  37.3 8.1 %all-to-all-done.1 = f32[16,1,576]{2,1,0:T(1,128)S(1)} async-done(((f32[16,1,576]{2,1,0:T(1,128)}), f32[16,1,576]{2,1,0:T(1,128)S(1)}, u32[]{:S(2)}, u32[]{:S(2)}) %all-to-all-start.1) | async-done | bytes 36896 | tf_op jit(solution)/shard_map/all_to_all | solution.py:31
  45.4 0.1 reduce.12
  45.5 0.1 squeeze_reshape_transpose.3
  45.6 1.9 fusion.40
  47.5 0.0 all-gather.9.cloned.1.call-start
  47.6 0.1 broadcast_in_dim.19
  47.7 35.8 %all_to_all.44 = bf16[16,1,128,192]{2,3,1,0:T(8,128)(2,1)S(1)} all-to-all(bf16[16,1,128,192]{2,3,1,0:T(8,128)(2,1)S(1)} %broadcast_in_dim.19), channel_id=1, replica_groups=mesh['cand'=16,'seq'=16] {'seq'}, dimensions={0} | all-to-all | bytes 1572864 | tf_op jit(solution)/shard_map/all_to_all | solution.py:31
  83.6 1.4 copy.33
  85.1 0.1 broadcast_multiply_fusion.2
  85.2 0.1 broadcast_multiply_fusion
  85.3 0.4 concatenate.44
  85.6 0.4 concatenate.43
  86.0 1.4 fusion.82
  87.4 2.2 fusion.81
  89.6 4.3 copy.29
  93.9 79.1 %all-gather.5.cloned.1.call-done = bf16[768,3072]{1,0:T(8,128)(2,1)} async-done(((bf16[48,3072]{1,0:T(8,128)(2,1)}), bf16[768,3072]{1,0:T(8,128)(2,1)}) %all-gather.5.cloned.1.call-update) | async-done | bytes 4718608 | tf_op jit(solution)/shard_map/all_gather | solution.py:185
  173.0 5.1 %fusion.5 = f32[768,3,128]{0,2,1:T(8,128)S(1)} fusion(bf16[3,128,3072]{2,1,0:T(8,128)(2,1)} %bitcast.240, bf16[768,3072]{1,0:T(8,128)(2,1)} %all-gather.5.cloned.1.call-done), kind=kOutput, calls=%fused_computation.10 | convolution fusion | flops 1811939328 | bytes 8257536 | tf_op jit(solution)/shard_map/dot_general | solution.py:189
  178.3 0.8 gather_fusion.1
  179.2 1.6 gather_fusion
  180.7 132.4 %all-gather.9.cloned.1.call-done = bf16[16,1,128,3072]{2,0,1,3:T(8,128)(2,1)} async-done(((bf16[16,1,128,192]{2,0,1,3:T(8,128)(2,1)}), bf16[16,1,128,3072]{2,0,1,3:T(8,128)(2,1)}) %all-gather.9.cloned.1.call-update) | async-done | bytes 12582928 | tf_op jit(solution)/shard_map/all_gather | solution.py:192
  313.1 7.0 %fusion.28 = bf16[6,16,8,128]{3,2,1,0:T(8,128)(2,1)S(1)} fusion(bf16[384,8,16,128]{3,2,1,0:T(8,128)(2,1)} %bitcast.237, bf16[1,48,3072]{2,1,0:T(8,128)(2,1)S(1)} %copy-done.15, f32[3072]{0:T(1024)S(1)} %get-tuple-element.23), kind=kOutput, calls=%fused_computation.28 | convolution fusion | flops 604520448 | bytes 13086720 | tf_op jit(solution)/shard_map/dot_general | solution.py:108
  320.1 0.7 copy.52
  320.9 4.4 all-to-all-start.4
  325.3 0.2 reduce-scatter.2.cloned.1.call-start
  325.5 0.2 fusion.66
  325.7 0.7 copy-done.10
  326.4 2.0 fusion.27
  328.4 6.9 %all-to-all-done.4 = bf16[48,16,128]{2,0,1:T(8,128)(2,1)S(1)} async-done(((bf16[48,16,128]{2,0,1:T(8,128)(2,1)}), bf16[48,16,128]{2,0,1:T(8,128)(2,1)S(1)}, u32[]{:S(2)}, u32[]{:S(2)}) %all-to-all-start.4) | async-done | bytes 196640 | tf_op jit(solution)/shard_map/all_to_all | solution.py:199
  335.3 2.6 multiply_reduce_fusion
  337.9 0.7 multiply_convert_fusion
  338.6 1.0 fusion.31
  339.6 0.5 convolution_multiply_fusion.1
  340.2 1.1 fusion.80
  341.3 1.6 gather_fusion.3
  342.8 1.6 gather_fusion.2
  344.4 1.7 multiply_reduce_fusion.2
  346.2 0.3 fusion.63
  346.5 0.1 pad_maximum_fusion
  346.6 1.2 copy-done.9
  347.9 4.3 convolution_convert_fusion
  352.2 1.1 convolution_convert_fusion.2
  353.3 3.5 all-to-all-start.2
  356.9 17.0 %copy.34 = bf16[16,1,128,3072]{3,2,0,1:T(8,128)(2,1)} copy(bf16[16,1,128,3072]{2,0,1,3:T(8,128)(2,1)} %all-gather.9.cloned.1.call-done) | data formatting | bytes 25165824 | tf_op jit(solution)/shard_map/all_gather | solution.py:192
  373.8 6.6 %fusion.19 = bf16[1,48,3072]{2,1,0:T(8,128)(2,1)} fusion(bf16[16,1,128,3072]{3,2,0,1:T(8,128)(2,1)} %copy.34, bf16[1,48,3072]{2,1,0:T(8,128)(2,1)S(1)} %copy-done.1, f32[3072]{0:T(1024)S(1)} %get-tuple-element.23, bf16[16,48,128]{2,1,0:T(8,128)(2,1)S(1)} %all-to-all-done.2), kind=kOutput, calls=%fused_computation.16 | convolution fusion | flops 604569600 | bytes 13381632 | tf_op jit(solution)/shard_map/dot_general | solution.py:195
  380.5 64.8 %reduce-scatter.2.cloned.1.call-done = bf16[48,3072]{1,0:T(8,128)(2,1)} async-done(((bf16[768,3072]{1,0:T(8,128)(2,1)}), bf16[48,3072]{1,0:T(8,128)(2,1)}) %reduce-scatter.2.cloned.1.call-update) | async-done | bytes 294928 | tf_op jit(solution)/shard_map/reduce_scatter | solution.py:201
  445.3 1.2 fusion.48
  446.5 2.0 fusion.45
  (62 shorter events, 0.4 us)
Async XLA Ops:
  7.2 1.9 copy-start
  7.2 40.4 %copy-start.17 = (bf16[1,128,192]{1,2,0:T(8,128)(2,1)S(1)}, bf16[1,128,192]{1,2,0:T(8,128)(2,1)}, u32[]{:S(2)}) copy-start(bf16[1,128,192]{1,2,0:T(8,128)(2,1)} %param.18) | copy-start | bytes 147460
  7.2 82.4 %all-gather.7.cloned.1.call-start = ((), (), s32[]{:S(2)}) async-start(), calls=%async_computation.7 | async-start | bytes 2506752 | tf_op jit(solution)/shard_map/all_gather | solution.py:188
  11.2 19.2 %all-to-all-start = ((bf16[16,2,288]{2,1,0:T(2,128)(2,1)}), bf16[16,2,288]{2,1,0:T(2,128)(2,1)S(1)}, u32[]{:S(2)}, u32[]{:S(2)}) async-start(bf16[16,2,288]{2,1,0:T(2,128)(2,1)} %reshape.1012), calls=%async_computation | async-start | bytes 49152 | tf_op jit(solution)/shard_map/all_to_all | solution.py:19
  31.2 14.3 %all-to-all-start.1 = ((f32[16,1,576]{2,1,0:T(1,128)}), f32[16,1,576]{2,1,0:T(1,128)S(1)}, u32[]{:S(2)}, u32[]{:S(2)}) async-start(f32[16,1,576]{2,1,0:T(1,128)} %broadcast_in_dim.16), calls=%async_computation.1 | async-start | bytes 81920 | tf_op jit(solution)/shard_map/all_to_all | solution.py:31
  37.2 135.8 %all-gather.5.cloned.1.call-start = ((), (), s32[]{:S(2)}) async-start(), calls=%async_computation.6 | async-start | bytes 5013504 | tf_op jit(solution)/shard_map/all_gather | solution.py:185
  47.5 265.6 %all-gather.9.cloned.1.call-start = ((), (), s32[]{:S(2)}) async-start(), calls=%async_computation.9 | async-start | bytes 13369344 | tf_op jit(solution)/shard_map/all_gather | solution.py:192
  47.5 37.5 %copy-start.18 = (s32[3,768]{1,0:T(4,128)S(1)}, s32[3,768]{1,0:T(4,128)}, u32[]{:S(2)}) copy-start(s32[3,768]{1,0:T(4,128)} %param.15) | copy-start | bytes 27652
  83.6 2.4 copy-start.20
  179.1 134.0 %copy-start.15 = (bf16[1,48,3072]{2,1,0:T(8,128)(2,1)S(1)}, bf16[1,48,3072]{2,1,0:T(8,128)(2,1)}, u32[]{:S(2)}) copy-start(bf16[1,48,3072]{2,1,0:T(8,128)(2,1)} %param.19) | copy-start | bytes 884740
  313.1 12.4 %copy-start.13 = (f32[128,768]{1,0:T(8,128)S(1)}, f32[128,768]{1,0:T(8,128)}, u32[]{:S(2)}) copy-start(f32[128,768]{1,0:T(8,128)} %gather_fusion) | copy-start | bytes 1179652
  313.1 12.4 %copy-start.19 = (f32[128]{0:T(128)S(1)}, f32[128]{0:T(128)}, u32[]{:S(2)}) copy-start(f32[128]{0:T(128)} %constant.63.clone) | copy-start | bytes 1540
  320.9 14.4 %all-to-all-start.4 = ((bf16[48,16,128]{2,0,1:T(8,128)(2,1)}), bf16[48,16,128]{2,0,1:T(8,128)(2,1)S(1)}, u32[]{:S(2)}, u32[]{:S(2)}) async-start(bf16[48,16,128]{2,0,1:T(8,128)(2,1)} %bitcast.224), calls=%async_computation.4 | async-start | bytes 393216 | tf_op jit(solution)/shard_map/all_to_all | solution.py:199
  325.3 120.0 %reduce-scatter.2.cloned.1.call-start = ((), (), s32[]{:S(2)}) async-start(), calls=%async_computation.8 | async-start | bytes 5013504 | tf_op jit(solution)/shard_map/reduce_scatter | solution.py:201
  325.7 0.7 copy-start.10
  335.3 2.6 copy-start.2
  338.5 1.6 copy-start.11
  338.6 1.6 copy-start.12
  340.2 1.1 copy-start.3
  342.8 1.6 copy-start.4
  344.4 1.8 copy-start.5
  344.4 1.8 copy-start.6
  344.4 1.8 copy-start.7
  344.4 1.8 copy-start.8
  344.4 2.1 copy-start.14
  346.1 1.7 copy-start.9
  353.3 20.5 %all-to-all-start.2 = ((bf16[16,48,128]{2,1,0:T(8,128)(2,1)}), bf16[16,48,128]{2,1,0:T(8,128)(2,1)S(1)}, u32[]{:S(2)}, u32[]{:S(2)}) async-start(bf16[16,48,128]{2,1,0:T(8,128)(2,1)} %convolution_convert_fusion.2), calls=%async_computation.2 | async-start | bytes 393216 | tf_op jit(solution)/shard_map/all_to_all | solution.py:194
  356.9 17.0 %copy-start.1 = (bf16[1,48,3072]{2,1,0:T(8,128)(2,1)S(1)}, bf16[1,48,3072]{2,1,0:T(8,128)(2,1)}, u32[]{:S(2)}) copy-start(bf16[1,48,3072]{2,1,0:T(8,128)(2,1)} %param.13) | copy-start | bytes 884740
  373.8 72.7 %copy-start.16 = (bf16[1,48,3072]{2,1,0:T(8,128)(2,1)S(1)}, bf16[1,48,3072]{2,1,0:T(8,128)(2,1)}, u32[]{:S(2)}) copy-start(bf16[1,48,3072]{2,1,0:T(8,128)(2,1)} %param.19) | copy-start | bytes 884740
Sparse Core Ops, SparseCore 0:
  10.7 70.0 all-gather.6
  83.2 89.8 all-gather.4
  175.8 137.3 all-gather.8
  352.3 92.9 reduce-scatter.1
where the time goes:
time: 456 us; the launch traced here: 455 us
  waiting for transfers between devices  298 us (65%)
  local copies, waits for them, and re-layouts  37.4 us (8%)
  blocking collectives  35.8 us (8%)
  matrix products  31.7 us (7%)
  starting transfers between devices  25.7 us (6%)
  between operations  14.2 us (3%)
  other arithmetic  12.7 us (3%)
    all_gather x1, waiting for transfers between devices, on_device(): w_all = lax.all_gather(w_heads, 'cand', axis=2, tiled=True)  132 us
    all_gather x1, waiting for transfers between devices, on_device(): gathered = lax.all_gather(modulated, 'seq', axis=0, tiled=True)  79.1 us
    reduce_scatter x1, waiting for transfers between devices, on_device(): lax.psum_scatter(times_transposed(lax.slice_in_dim(d_projected, 0, rows_l...  64.8 us
    all_to_all x1, blocking collectives, from_everyone(): return lax.all_to_all(copies, axis, split_axis=0, concat_axis=0, tiled=True)  35.8 us
    all_gather x1, local copies, waits for them, and re-layouts, on_device(): w_all = lax.all_gather(w_heads, 'cand', axis=2, tiled=True)  17 us
    all_to_all x1, starting transfers between devices, summed_on_arrival(): parts = lax.all_to_all(in_blocks(value, dim, size), axis, 0, 0, tiled=True)  11.4 us
    dot_general x2, matrix products, times_transposed(): lax.dot_general(left, right, (((1,), (1,)), ((), ())), preferred_element_...  11.3 us
  transfers between devices with their start and end apart: 8, of which 6 were waited for; matrix products, arithmetic and copies ran while one was open for 12% of the time, Pallas kernels for 0%

commit v1 on v0

--- a/solution.py
+++ b/solution.py
@@ -182,7 +182,9 @@
     latent_rows = latent[0].astype(jnp.float32)
     normed, inverse_std = layer_norm(latent_rows)
     modulated = (normed * (1.0 + scale_vec) + shift_vec).astype(jnp.bfloat16)
-    gathered = lax.all_gather(modulated, "seq", axis=0, tiled=True)
+    gathered = jnp.concatenate(
+        lax.all_to_all(jnp.stack([modulated] * lax.axis_size("seq")), "seq", 0, 0), axis=0
+    )
     length = gathered.shape[0]
     tables = rope_tables(positions, HEAD)
     w_full = lax.all_gather(input_weight, "cand", axis=0, tiled=True).reshape(width, group_cols)

time: 456 us -> 423 us (0.928)
  waiting for transfers between devices: 298 us -> 251 us
  starting transfers between devices: 25.7 us -> 42.5 us
    all_to_all x0 -> x1, waiting for transfers between devices: none -> 163 us  [on_device(): lax.all_to_all(jnp.stack([modulated] * lax.axis_size('seq')), 'seq', 0, 0)]
    all_gather x1, waiting for transfers between devices: 132 us -> 0.01 us  [on_device(): w_all = lax.all_gather(w_heads, 'cand', axis=2, tiled=True)]
    all_gather x1 -> x0, waiting for transfers between devices: 79.1 us -> none  [on_device(): gathered = lax.all_gather(modulated, 'seq', axis=0, tiled=True)]
    all_to_all x1, starting transfers between devices: 4.39 us -> 20.6 us  [on_device(): lax.all_to_all(d_tokens, 'seq', split_axis=1, concat_axis=0, tiled=True)]
    all_to_all x0 -> x1, starting transfers between devices: none -> 4.7 us  [on_device(): lax.all_to_all(jnp.stack([modulated] * lax.axis_size('seq')), 'seq', 0, 0)]
  transfers between devices with their start and end apart: 8 -> 8, of which waited for: 6 -> 5; matrix products, arithmetic and copies ran while one was open for 12% -> 13% of each run, Pallas kernels for 0% -> 0%
where the time goes in v1:
time: 423 us; the launch traced here: 421 us
  waiting for transfers between devices  251 us (59%)
  starting transfers between devices  42.5 us (10%)
  local copies, waits for them, and re-layouts  40.2 us (10%)
  blocking collectives  33.3 us (8%)
  matrix products  31.3 us (7%)
  between operations  14.2 us (3%)
  other arithmetic  8.42 us (2%)
    all_to_all x1, waiting for transfers between devices, on_device(): lax.all_to_all(jnp.stack([modulated] * lax.axis_size('seq')), 'seq', 0, 0)  163 us
    reduce_scatter x1, waiting for transfers between devices, on_device(): lax.psum_scatter(times_transposed(lax.slice_in_dim(d_projected, 0, rows_l...  63.3 us
    all_to_all x1, blocking collectives, from_everyone(): return lax.all_to_all(copies, axis, split_axis=0, concat_axis=0, tiled=True)  33.3 us
    all_to_all x1, starting transfers between devices, on_device(): lax.all_to_all(d_tokens, 'seq', split_axis=1, concat_axis=0, tiled=True)  20.6 us
    all_gather x1, local copies, waits for them, and re-layouts, on_device(): w_all = lax.all_gather(w_heads, 'cand', axis=2, tiled=True)  16.7 us
    dot_general x2, matrix products, times_transposed(): lax.dot_general(left, right, (((1,), (1,)), ((), ())), preferred_element_...  11.3 us
    all_to_all x1, starting transfers between devices, summed_on_arrival(): parts = lax.all_to_all(in_blocks(value, dim, size), axis, 0, 0, tiled=True)  8.75 us
    all_to_all x1, waiting for transfers between devices, summed_on_arrival(): parts = lax.all_to_all(in_blocks(value, dim, size), axis, 0, 0, tiled=True)  8.61 us
  transfers between devices with their start and end apart: 8, of which 5 were waited for; matrix products, arithmetic and copies ran while one was open for 13% of the time, Pallas kernels for 0%

profile of v1, /device:TPU:4, one launch (start us, length us, event | category | flops | bytes accessed | tf_op | source)
XLA Modules:
  0.0 420.9 jit_solution(5003429844576711342)
XLA Ops:
  7.2 0.0 all-gather.4.cloned.1.call-start
  7.2 0.7 all-gather.4.cloned.1.call-update
  7.9 0.0 all-gather.6.cloned.1.call-start
  8.0 0.9 broadcast_in_dim.19
  8.9 33.3 %all_to_all.49 = bf16[16,1,128,192]{2,3,1,0:T(8,128)(2,1)S(1)} all-to-all(bf16[16,1,128,192]{2,3,1,0:T(8,128)(2,1)S(1)} %broadcast_in_dim.19), channel_id=1, replica_groups=mesh['cand'=16,'seq'=16] {'seq'}, dimensions={0} | all-to-all | bytes 1572864 | tf_op jit(solution)/shard_map/all_to_all | solution.py:31
  42.3 1.4 copy.33
  43.7 0.0 all-gather.6.cloned.1.call-update
  43.7 0.4 multiply_cosine_fusion
  44.2 0.2 fusion.30
  44.4 0.5 broadcast.545
  44.9 0.7 reduce.19
  45.6 0.7 reshape.1043
  46.3 8.7 %all-to-all-start = ((bf16[16,2,288]{2,1,0:T(2,128)(2,1)}), bf16[16,2,288]{2,1,0:T(2,128)(2,1)S(1)}, u32[]{:S(2)}, u32[]{:S(2)}) async-start(bf16[16,2,288]{2,1,0:T(2,128)(2,1)} %reshape.1043), calls=%async_computation | async-start | bytes 49152 | tf_op jit(solution)/shard_map/all_to_all | solution.py:19
  55.1 0.2 convert_reduce_fusion
  55.2 0.3 fusion.41
  55.5 8.6 %all-to-all-done = bf16[16,2,288]{2,1,0:T(2,128)(2,1)S(1)} async-done(((bf16[16,2,288]{2,1,0:T(2,128)(2,1)}), bf16[16,2,288]{2,1,0:T(2,128)(2,1)S(1)}, u32[]{:S(2)}, u32[]{:S(2)}) %all-to-all-start) | async-done | bytes 18464 | tf_op jit(solution)/shard_map/all_to_all | solution.py:19
  64.1 0.1 reshape.1044
  64.2 0.1 convert_reduce_fusion.1
  64.2 0.6 broadcast_in_dim.16
  64.9 4.6 %all-to-all-start.1 = ((f32[16,1,576]{2,1,0:T(1,128)}), f32[16,1,576]{2,1,0:T(1,128)S(1)}, u32[]{:S(2)}, u32[]{:S(2)}) async-start(f32[16,1,576]{2,1,0:T(1,128)} %broadcast_in_dim.16), calls=%async_computation.1 | async-start | bytes 81920 | tf_op jit(solution)/shard_map/all_to_all | solution.py:31
  69.5 8.2 %all-to-all-done.1 = f32[16,1,576]{2,1,0:T(1,128)S(1)} async-done(((f32[16,1,576]{2,1,0:T(1,128)}), f32[16,1,576]{2,1,0:T(1,128)S(1)}, u32[]{:S(2)}, u32[]{:S(2)}) %all-to-all-start.1) | async-done | bytes 36896 | tf_op jit(solution)/shard_map/all_to_all | solution.py:31
  77.7 0.1 reduce.12
  77.8 0.1 squeeze_reshape_transpose.3
  77.9 0.2 fusion.59
  78.1 2.7 stack.17
  80.9 4.7 %all-to-all-start.2 = ((bf16[16,48,3072]{2,1,0:T(8,128)(2,1)}), bf16[16,48,3072]{2,1,0:T(8,128)(2,1)}, u32[]{:S(2)}, u32[]{:S(2)}) async-start(bf16[16,48,3072]{2,1,0:T(8,128)(2,1)} %stack.17), calls=%async_computation.2 | async-start | bytes 9437184 | tf_op jit(solution)/shard_map/all_to_all | solution.py:186
  85.6 0.1 broadcast_multiply_fusion.2
  85.7 0.1 broadcast_multiply_fusion
  85.8 0.4 concatenate.43
  86.2 0.4 concatenate.44
  86.6 1.4 fusion.82
  88.0 2.2 fusion.81
  90.2 4.4 %copy.29 = bf16[384,3072]{1,0:T(8,128)(2,1)} copy(bf16[384,3072]{0,1:T(8,128)(2,1)} %bitcast.236) | data formatting | bytes 4718592 | tf_op jit(solution)/shard_map/dot_general | solution.py:191
  94.6 163.1 %all-to-all-done.2 = bf16[16,48,3072]{2,1,0:T(8,128)(2,1)} async-done(((bf16[16,48,3072]{2,1,0:T(8,128)(2,1)}), bf16[16,48,3072]{2,1,0:T(8,128)(2,1)}, u32[]{:S(2)}, u32[]{:S(2)}) %all-to-all-start.2) | async-done | bytes 4718624 | tf_op jit(solution)/shard_map/all_to_all | solution.py:186
  257.6 5.4 %fusion.83 = f32[768,3,128]{0,2,1:T(8,128)S(1)} fusion(bf16[768,3072,1]{1,0,2:T(8,128)(2,1)} %bitcast.4, bf16[3,128,3072]{2,1,0:T(8,128)(2,1)} %bitcast.237), kind=kOutput, calls=%fused_computation.130 | convolution fusion | flops 1811939328 | bytes 8257536 | tf_op jit(solution)/shard_map/dot_general | solution.py:191
  263.2 0.8 gather_fusion.1
  264.0 1.6 gather_fusion
  265.6 7.0 %fusion.26 = bf16[6,16,8,128]{3,2,1,0:T(8,128)(2,1)S(1)} fusion(bf16[384,8,16,128]{3,2,1,0:T(8,128)(2,1)} %bitcast.234, bf16[1,48,3072]{2,1,0:T(8,128)(2,1)S(1)} %copy-done.16, f32[3072]{0:T(1024)S(1)} %get-tuple-element.23), kind=kOutput, calls=%fused_computation.26 | convolution fusion | flops 604520448 | bytes 13086720 | tf_op jit(solution)/shard_map/dot_general | solution.py:108
  272.6 0.7 copy.52
  273.3 20.6 %all-to-all-start.5 = ((bf16[48,16,128]{2,0,1:T(8,128)(2,1)}), bf16[48,16,128]{2,0,1:T(8,128)(2,1)S(1)}, u32[]{:S(2)}, u32[]{:S(2)}) async-start(bf16[48,16,128]{2,0,1:T(8,128)(2,1)} %bitcast.221), calls=%async_computation.5 | async-start | bytes 393216 | tf_op jit(solution)/shard_map/all_to_all | solution.py:201
  294.0 0.2 reduce-scatter.2.cloned.1.call-start
  294.2 0.2 fusion.66
  294.4 2.0 fusion.25
  296.4 7.0 %all-to-all-done.5 = bf16[48,16,128]{2,0,1:T(8,128)(2,1)S(1)} async-done(((bf16[48,16,128]{2,0,1:T(8,128)(2,1)}), bf16[48,16,128]{2,0,1:T(8,128)(2,1)S(1)}, u32[]{:S(2)}, u32[]{:S(2)}) %all-to-all-start.5) | async-done | bytes 196640 | tf_op jit(solution)/shard_map/all_to_all | solution.py:201
  303.4 2.6 multiply_reduce_fusion
  306.0 0.7 multiply_convert_fusion
  306.7 0.5 convolution_multiply_fusion.1
  307.3 1.1 fusion.80
  308.4 1.6 gather_fusion.3
  310.0 1.6 gather_fusion.2
  311.5 1.7 multiply_reduce_fusion.2
  313.3 0.4 fusion.29
  313.7 0.3 fusion.63
  314.0 0.1 pad_maximum_fusion
  314.1 1.3 copy-done.11
  315.4 4.3 %convolution_convert_fusion = bf16[768,3072]{1,0:T(8,128)(2,1)} fusion(bf16[768,384]{0,1:T(8,128)(2,1)S(1)} %bitcast.240, bf16[3072,1,384]{2,0,1:T(8,128)(2,1)S(1)} %copy-done.11), kind=kOutput, calls=%fused_computation.9 | convolution fusion | flops 1814298624 | bytes 7667712 | tf_op jit(solution)/shard_map/dot_general | solution.py:108
  319.7 0.0 reduce-scatter.2.cloned.1.call-update
  319.7 1.1 convolution_convert_fusion.2
  320.8 3.5 all-to-all-start.3
  324.4 16.7 %copy.34 = bf16[16,1,128,3072]{3,2,0,1:T(8,128)(2,1)} copy(bf16[16,1,128,3072]{2,0,1,3:T(8,128)(2,1)} %all-gather.6.cloned.1.call-done) | data formatting | bytes 25165824 | tf_op jit(solution)/shard_map/all_gather | solution.py:194
  341.1 6.7 %fusion.17 = bf16[1,48,3072]{2,1,0:T(8,128)(2,1)} fusion(bf16[16,1,128,3072]{3,2,0,1:T(8,128)(2,1)} %copy.34, bf16[1,48,3072]{2,1,0:T(8,128)(2,1)S(1)} %copy-done.3, f32[3072]{0:T(1024)S(1)} %get-tuple-element.23, bf16[16,48,128]{2,1,0:T(8,128)(2,1)S(1)} %all-to-all-done.3), kind=kOutput, calls=%fused_computation.14 | convolution fusion | flops 604569600 | bytes 13381632 | tf_op jit(solution)/shard_map/dot_general | solution.py:197
  347.8 63.3 %reduce-scatter.2.cloned.1.call-done = bf16[48,3072]{1,0:T(8,128)(2,1)} async-done(((bf16[768,3072]{1,0:T(8,128)(2,1)}), bf16[48,3072]{1,0:T(8,128)(2,1)}) %reduce-scatter.2.cloned.1.call-update) | async-done | bytes 294928 | tf_op jit(solution)/shard_map/reduce_scatter | solution.py:203
  411.1 1.2 fusion.47
  412.3 2.0 fusion.40
  (64 shorter events, 0.4 us)
Async XLA Ops:
  7.2 37.0 %copy-start = (bf16[192,576]{1,0:T(8,128)(2,1)S(1)}, bf16[192,576]{1,0:T(8,128)(2,1)}, u32[]{:S(2)}) copy-start(bf16[192,576]{1,0:T(8,128)(2,1)} %param.16) | copy-start | bytes 663556
  7.2 83.0 %all-gather.4.cloned.1.call-start = ((), (), s32[]{:S(2)}) async-start(), calls=%async_computation.7 | async-start | bytes 2506752 | tf_op jit(solution)/shard_map/all_gather | solution.py:190
  7.9 257.7 %all-gather.6.cloned.1.call-start = ((), (), s32[]{:S(2)}) async-start(), calls=%async_computation.9 | async-start | bytes 13369344 | tf_op jit(solution)/shard_map/all_gather | solution.py:194
  8.0 35.8 %copy-start.21 = (s32[16]{0:T(128)S(1)}, s32[16]{0:T(128)}, u32[]{:S(2)}) copy-start(s32[16]{0:T(128)} %param.14) | copy-start | bytes 196
  8.9 46.1 %copy-start.2 = (bf16[1,48,3072]{2,1,0:T(8,128)(2,1)S(1)}, bf16[1,48,3072]{2,1,0:T(8,128)(2,1)}, u32[]{:S(2)}) copy-start(bf16[1,48,3072]{2,1,0:T(8,128)(2,1)} %param.13) | copy-start | bytes 884740
  46.3 17.8 %all-to-all-start = ((bf16[16,2,288]{2,1,0:T(2,128)(2,1)}), bf16[16,2,288]{2,1,0:T(2,128)(2,1)S(1)}, u32[]{:S(2)}, u32[]{:S(2)}) async-start(bf16[16,2,288]{2,1,0:T(2,128)(2,1)} %reshape.1043), calls=%async_computation | async-start | bytes 49152 | tf_op jit(solution)/shard_map/all_to_all | solution.py:19
  64.9 12.8 %all-to-all-start.1 = ((f32[16,1,576]{2,1,0:T(1,128)}), f32[16,1,576]{2,1,0:T(1,128)S(1)}, u32[]{:S(2)}, u32[]{:S(2)}) async-start(f32[16,1,576]{2,1,0:T(1,128)} %broadcast_in_dim.16), calls=%async_computation.1 | async-start | bytes 81920 | tf_op jit(solution)/shard_map/all_to_all | solution.py:31
  80.8 4.7 %copy-start.18 = (s32[3,768]{1,0:T(4,128)S(1)}, s32[3,768]{1,0:T(4,128)}, u32[]{:S(2)}) copy-start(s32[3,768]{1,0:T(4,128)} %param.15) | copy-start | bytes 27652
  80.9 5.7 %copy-start.20 = (s32[128]{0:T(128)S(1)}, s32[128]{0:T(128)}, u32[]{:S(2)}) copy-start(s32[128]{0:T(128)} %constant.69) | copy-start | bytes 1540
  80.9 176.8 %all-to-all-start.2 = ((bf16[16,48,3072]{2,1,0:T(8,128)(2,1)}), bf16[16,48,3072]{2,1,0:T(8,128)(2,1)}, u32[]{:S(2)}, u32[]{:S(2)}) async-start(bf16[16,48,3072]{2,1,0:T(8,128)(2,1)} %stack.17), calls=%async_computation.2 | async-start | bytes 9437184 | tf_op jit(solution)/shard_map/all_to_all | solution.py:186
  264.0 1.6 copy-start.16
  265.6 28.6 %copy-start.13 = (f32[128,768]{1,0:T(8,128)S(1)}, f32[128,768]{1,0:T(8,128)}, u32[]{:S(2)}) copy-start(f32[128,768]{1,0:T(8,128)} %gather_fusion) | copy-start | bytes 1179652
  265.6 28.6 %copy-start.19 = (f32[128]{0:T(128)S(1)}, f32[128]{0:T(128)}, u32[]{:S(2)}) copy-start(f32[128]{0:T(128)} %constant.63.clone) | copy-start | bytes 1540
  273.3 30.1 %all-to-all-start.5 = ((bf16[48,16,128]{2,0,1:T(8,128)(2,1)}), bf16[48,16,128]{2,0,1:T(8,128)(2,1)S(1)}, u32[]{:S(2)}, u32[]{:S(2)}) async-start(bf16[48,16,128]{2,0,1:T(8,128)(2,1)} %bitcast.221), calls=%async_computation.5 | async-start | bytes 393216 | tf_op jit(solution)/shard_map/all_to_all | solution.py:201
  294.0 117.1 %reduce-scatter.2.cloned.1.call-start = ((), (), s32[]{:S(2)}) async-start(), calls=%async_computation.8 | async-start | bytes 5013504 | tf_op jit(solution)/shard_map/reduce_scatter | solution.py:203
  303.4 2.6 copy-start.14
  303.4 2.6 copy-start.4
  306.0 1.2 copy-start.12
  307.2 1.1 copy-start.5
  310.0 1.6 copy-start.6
  311.5 1.8 copy-start.15
  311.5 2.1 copy-start.7
  311.5 2.2 copy-start.8
  311.5 2.2 copy-start.9
  311.5 2.2 copy-start.10
  313.7 1.7 copy-start.11
  320.8 20.3 %all-to-all-start.3 = ((bf16[16,48,128]{2,1,0:T(8,128)(2,1)}), bf16[16,48,128]{2,1,0:T(8,128)(2,1)S(1)}, u32[]{:S(2)}, u32[]{:S(2)}) async-start(bf16[16,48,128]{2,1,0:T(8,128)(2,1)} %convolution_convert_fusion.2), calls=%async_computation.3 | async-start | bytes 393216 | tf_op jit(solution)/shard_map/all_to_all | solution.py:196
  324.4 16.8 %copy-start.3 = (bf16[1,48,3072]{2,1,0:T(8,128)(2,1)S(1)}, bf16[1,48,3072]{2,1,0:T(8,128)(2,1)}, u32[]{:S(2)}) copy-start(bf16[1,48,3072]{2,1,0:T(8,128)(2,1)} %param.13) | copy-start | bytes 884740
  341.1 71.2 %copy-start.17 = (bf16[1,48,3072]{2,1,0:T(8,128)(2,1)S(1)}, bf16[1,48,3072]{2,1,0:T(8,128)(2,1)}, u32[]{:S(2)}) copy-start(bf16[1,48,3072]{2,1,0:T(8,128)(2,1)} %param.19) | copy-start | bytes 884740
  341.1 73.2 %copy-start.1 = (bf16[192,576]{1,0:T(8,128)(2,1)S(1)}, bf16[192,576]{1,0:T(8,128)(2,1)}, u32[]{:S(2)}) copy-start(bf16[192,576]{1,0:T(8,128)(2,1)} %param.16) | copy-start | bytes 663556
Sparse Core Ops, SparseCore 0:
  10.7 67.6 all-gather.3
  81.2 179.5 all-gather.5
  319.8 91.2 reduce-scatter.1
